TPU v7x, 32 devices: a whole 2x2x4 slice. The times are simulated.
32 devices in a mesh: dom: 16 (over z, y, x), col: 2 (over core).
Axes of the slice: x: 2, y: 2, z: 4, core: 2. Of those that a mesh axis runs over, the one named last changes fastest.
Arguments:
- features: bfloat16 [16384, 256], P(('dom', 'col')), may hold values from -6 to 6
- weight: bfloat16 [256, 256], replicated, may hold values from -0.375 to 0.375
- cotangent: bfloat16 [16384, 256], P(('dom', 'col')), may hold values from -6 to 6
- tile_values: bfloat16 [1280, 128, 128], P(('dom', 'col')), may hold values from -0.15625 to 0.15625
- tile_rows: int32 [1280], P(('dom', 'col')), may hold values from 0 to 7
- tile_cols: int32 [1280], P(('dom', 'col')), may hold values from 0 to 19, as said below
- tile_count: int32 [32], P(('dom', 'col')), may hold values from 20 to 40, as said below
- send_blocks: int32 [32, 16], P(('dom', 'col')), may hold values from 0 to 3
Outputs:
- output_rows: bfloat16 [16384, 256], P(('dom', 'col'))
- feature_grad: bfloat16 [16384, 256], P(('dom', 'col'))
- weight_grad: float32 [256, 256], replicated
Inputs may be any that keep to these rules, and one draw needn't show every extreme that they name: `tile_cols`: A value v below 4 names the device's own row block v; a value 4 + s names the row block that the device of partition s with the same col index sends to this partition; no receive slot is named by two tiles of one device. Only the first tile_count slots of a device's tiles are live; some device has all 40 live.
All inputs are finite; a program needn't handle non-finite values.
Results may differ from a plain program's by a relative error of at most 0.0049.
Values may be sent and summed in bfloat16 or wider, within the bound.
A program may use at most 128 MiB of HBM per device.

v0:
```python
import jax
import jax.numpy as jnp
from jax import lax
from jax.sharding import PartitionSpec as P


def local(features, weight, cotangent, tile_values, tile_rows, tile_cols, tile_count, send_blocks):
    block_size = tile_values.shape[1]
    half_blocks = features.shape[0] // block_size
    width_in = features.shape[1]
    peer_count = send_blocks.shape[1]
    all_blocks = half_blocks * lax.axis_size("col")
    node_total = features.shape[0] * lax.axis_size("col") * lax.axis_size("dom")
    own_blocks = features.reshape(half_blocks, block_size, width_in)
    outgoing = own_blocks[send_blocks[0]]
    incoming = lax.all_to_all(outgoing, "dom", split_axis=0, concat_axis=0, tiled=True)
    sources = jnp.concatenate([own_blocks, incoming], axis=0)
    live_bool = jnp.arange(tile_values.shape[0], dtype=jnp.int32) < tile_count[0]
    live_mask = live_bool.astype(jnp.bfloat16)
    masked_tiles = tile_values * live_mask[:, None, None]
    picked = sources[tile_cols]
    products = jnp.einsum("tij,tjf->tif", masked_tiles, picked, preferred_element_type=jnp.float32)
    partial_value = jax.ops.segment_sum(products, tile_rows, num_segments=all_blocks)
    summed = lax.psum_scatter(partial_value, "col", scatter_dimension=0, tiled=True)
    hidden = summed.astype(jnp.bfloat16).reshape(half_blocks * block_size, width_in)
    output_rows = jnp.dot(hidden, weight, preferred_element_type=jnp.float32).astype(jnp.bfloat16)
    own_grad = lax.dot_general(
        cotangent, weight, (((1,), (1,)), ((), ())), preferred_element_type=jnp.float32
    ).astype(jnp.bfloat16)
    own_grad = own_grad.reshape(half_blocks, block_size, width_in)
    grad_blocks = lax.all_gather(own_grad, "col", axis=0, tiled=True)
    chosen = grad_blocks[tile_rows]
    back_terms = jnp.einsum(
        "tji,tjf->tif", masked_tiles, chosen, preferred_element_type=jnp.float32
    )
    spread = jax.ops.segment_sum(back_terms, tile_cols, num_segments=half_blocks + peer_count)
    returned = lax.all_to_all(spread[half_blocks:], "dom", split_axis=0, concat_axis=0, tiled=True)
    grad_total = spread[:half_blocks] + jax.ops.segment_sum(
        returned, send_blocks[0], num_segments=half_blocks
    )
    feature_grad = grad_total.astype(jnp.bfloat16).reshape(half_blocks * block_size, width_in)
    local_weight = lax.dot_general(
        hidden, cotangent, (((0,), (0,)), ((), ())), preferred_element_type=jnp.float32
    )
    local_weight = local_weight * jnp.float32(1.0 / node_total**0.5)
    col_share = lax.psum_scatter(local_weight, "col", scatter_dimension=0, tiled=True)
    dom_share = lax.psum(col_share, "dom")
    weight_grad = lax.all_gather(dom_share, "col", axis=0, tiled=True)
    return (output_rows, feature_grad, weight_grad)


def solution(mesh):
    return jax.shard_map(
        local,
        mesh=mesh,
        in_specs=(
            P(("dom", "col"), None),
            P(),
            P(("dom", "col"), None),
            P(("dom", "col"), None, None),
            P(("dom", "col")),
            P(("dom", "col")),
            P(("dom", "col")),
            P(("dom", "col"), None),
        ),
        out_specs=(P(("dom", "col"), None), P(("dom", "col"), None), P()),
        check_vma=False,
    )
```

profile of v0, /device:TPU:0, one launch (start us, length us, event | category | flops | bytes accessed | tf_op | source)
XLA Modules:
  0.0 214.5 jit_solution(6143368337666922137)
XLA Ops:
  7.2 0.7 fusion.6
  7.9 2.6 %gather_fusion = bf16[16,128,256]{2,1,0:T(8,128)(2,1)} fusion(bf16[4,128,256]{2,1,0:T(8,128)(2,1)} %bitcast.19, s32[1024]{0:T(1024)S(1)} %pad_clamp_fusion.2), kind=kCustom, calls=%fused_computation | custom fusion | bytes 2097216 | tf_op jit(solution)/shard_map/gather | solution.py:15
  10.5 8.4 %all-to-all-start = ((bf16[16,128,256]{2,1,0:T(8,128)(2,1)}), bf16[16,128,256]{2,1,0:T(8,128)(2,1)}, u32[]{:S(2)}, u32[]{:S(2)}) async-start(bf16[16,128,256]{2,1,0:T(8,128)(2,1)} %gather_fusion), calls=%async_computation | async-start | bytes 2097152 | tf_op jit(solution)/shard_map/all_to_all | solution.py:16
  19.6 0.3 convolution_convert_fusion
  19.9 2.2 %all_gather.6 = bf16[8,128,256]{2,1,0:T(8,128)(2,1)S(1)} all-gather(bf16[4,128,256]{2,1,0:T(8,128)(2,1)S(1)} %bitcast.23), channel_id=1, replica_groups=mesh['dom'=16,'col'=2] {'col'}, dimensions={0}, use_global_device_ids=true | all-gather | bytes 786432 | tf_op jit(solution)/shard_map/all_gather | solution.py:31
  22.0 0.7 gather_fusion.2
  22.8 4.9 %fusion = f32[40,128,256]{2,1,0:T(8,128)} fusion(bf16[40,128,256]{2,1,0:T(8,128)(2,1)S(1)} %gather_fusion.2, bf16[40,128,128]{2,1,0:T(8,128)(2,1)} %param.11, bf16[40]{0:T(256)(128)(2,1)S(1)} %compare_convert_fusion), kind=kOutput, calls=%fused_computation.10 | convolution fusion | flops 336199680 | bytes 9175120 | tf_op jit(solution)/shard_map/tji,tjf->tif/dot_general | solution.py:33
  27.7 0.3 broadcast_in_dim.24
  28.0 0.4 copy-done.6
  28.4 9.1 %scatter_fusion.1 = f32[20,128,256]{2,1,0:T(8,128)S(1)} fusion(f32[20,128,256]{2,1,0:T(8,128)S(1)} %broadcast_in_dim.24, s32[40]{0:T(128)S(1)} %copy-done.6, f32[40,128,256]{2,1,0:T(8,128)} %fusion), kind=kCustom, calls=%fused_computation.4 | custom fusion | flops 1310720 | bytes 15728800 | tf_op jit(solution)/shard_map/scatter-add | solution.py:36
  37.4 1.8 slice.15
  39.2 4.1 %all-to-all-done = bf16[16,128,256]{2,1,0:T(8,128)(2,1)} async-done(((bf16[16,128,256]{2,1,0:T(8,128)(2,1)}), bf16[16,128,256]{2,1,0:T(8,128)(2,1)}, u32[]{:S(2)}, u32[]{:S(2)}) %all-to-all-start) | async-done | bytes 1048608 | tf_op jit(solution)/shard_map/all_to_all | solution.py:16
  43.3 5.9 %all-to-all-start.1 = ((f32[16,128,256]{2,1,0:T(8,128)}), f32[16,128,256]{2,1,0:T(8,128)}, u32[]{:S(2)}, u32[]{:S(2)}) async-start(f32[16,128,256]{2,1,0:T(8,128)} %slice.15), calls=%async_computation.2 | async-start | bytes 4194304 | tf_op jit(solution)/shard_map/all_to_all | solution.py:37
  49.4 1.3 pad_maximum_fusion
  50.7 2.4 %gather_fusion.1 = bf16[40,128,256]{2,1,0:T(8,128)(2,1)} fusion(bf16[20,128,256]{2,1,0:T(8,128)(2,1)S(1)} %pad_maximum_fusion, s32[1024]{0:T(1024)S(1)} %pad_clamp_fusion.1), kind=kCustom, calls=%fused_computation.1 | custom fusion | bytes 5243040 | tf_op jit(solution)/shard_map/gather | solution.py:21
  53.1 4.9 %fusion.2 = f32[40,128,256]{2,1,0:T(8,128)} fusion(bf16[40,128,256]{2,1,0:T(8,128)(2,1)} %gather_fusion.1, bf16[40,128,128]{2,1,0:T(8,128)(2,1)S(1)} %copy-done.4, bf16[40]{0:T(256)(128)(2,1)S(1)} %compare_convert_fusion), kind=kOutput, calls=%fused_computation.12 | convolution fusion | flops 336199680 | bytes 9175120 | tf_op jit(solution)/shard_map/tij,tjf->tif/dot_general | solution.py:22
  58.1 0.1 broadcast_in_dim.21
  58.1 9.0 %scatter_fusion = f32[8,128,256]{2,1,0:T(8,128)S(1)} fusion(f32[8,128,256]{2,1,0:T(8,128)S(1)} %broadcast_in_dim.21, s32[40]{0:T(128)S(1)} %copy-done.7, f32[40,128,256]{2,1,0:T(8,128)} %fusion.2), kind=kCustom, calls=%fused_computation.3 | custom fusion | flops 1310720 | bytes 15728800 | tf_op jit(solution)/shard_map/scatter-add | solution.py:23
  67.2 1.1 copy-done.1
  68.3 0.0 reduce-scatter.5.cloned.1.call-start
  68.4 9.7 %reduce-scatter.3.cloned.1.call-done = f32[4,128,256]{2,1,0:T(8,128)} async-done(((f32[8,128,256]{2,1,0:T(8,128)}), f32[4,128,256]{2,1,0:T(8,128)}) %reduce-scatter.3.cloned.1.call-update) | async-done | bytes 524304 | tf_op jit(solution)/shard_map/reduce_scatter | solution.py:24
  78.1 1.1 convert_element_type.20
  79.1 1.0 convolution_multiply_fusion
  80.1 0.0 all-reduce.2.cloned.1.call-start
  80.2 1.1 slice.14
  81.3 10.0 %all-to-all-done.1 = f32[16,128,256]{2,1,0:T(8,128)} async-done(((f32[16,128,256]{2,1,0:T(8,128)}), f32[16,128,256]{2,1,0:T(8,128)}, u32[]{:S(2)}, u32[]{:S(2)}) %all-to-all-start.1) | async-done | bytes 2097184 | tf_op jit(solution)/shard_map/all_to_all | solution.py:37
  91.2 3.5 %scatter_fusion.2 = f32[4,128,256]{2,1,0:T(8,128)S(1)} fusion(f32[4,128,256]{2,1,0:T(8,128)S(1)} %slice.14, s32[16]{0:T(128)S(1)} %bitcast.25, f32[16,128,256]{2,1,0:T(8,128)} %all-to-all-done.1), kind=kCustom, calls=%fused_computation.5 | custom fusion | flops 524288 | bytes 6291520 | tf_op jit(solution)/shard_map/scatter-add | solution.py:38
  94.7 0.7 convert_element_type.23
  95.5 0.9 convolution_convert_fusion.1
  96.4 108.7 %all-reduce.2.cloned.1.call-done = f32[128,256]{1,0:T(8,128)} async-done(((f32[128,256]{1,0:T(8,128)}), f32[128,256]{1,0:T(8,128)}) %all-reduce.2.cloned.1.call-update) | async-done | bytes 131088 | tf_op jit(solution)/shard_map/psum | solution.py:47
  205.1 2.2 %all_gather.7 = f32[256,256]{1,0:T(8,128)S(1)} all-gather(f32[128,256]{1,0:T(8,128)} %all-reduce.2.cloned.1.call-done), channel_id=1, replica_groups=mesh['dom'=16,'col'=2] {'col'}, dimensions={0}, use_global_device_ids=true | all-gather | bytes 393216 | tf_op jit(solution)/shard_map/all_gather | solution.py:48
  207.3 0.7 copy.20
  (27 shorter events, 0.2 us)
Async XLA Ops:
  7.2 12.4 %copy-start = (bf16[512,256]{1,0:T(8,128)(2,1)S(1)}, bf16[512,256]{1,0:T(8,128)(2,1)}, u32[]{:S(2)}) copy-start(bf16[512,256]{1,0:T(8,128)(2,1)} %param.10) | copy-start | bytes 786436
  7.2 12.4 %copy-start.7 = (s32[40]{0:T(128)S(1)}, s32[40]{0:T(128)}, u32[]{:S(2)}) copy-start(s32[40]{0:T(128)} %param.12) | copy-start | bytes 484
  7.2 12.4 %copy-start.5 = (bf16[256,256]{1,0:T(8,128)(2,1)S(1)}, bf16[256,256]{1,0:T(8,128)(2,1)}, u32[]{:S(2)}) copy-start(bf16[256,256]{1,0:T(8,128)(2,1)} %param.9) | copy-start | bytes 393220
  10.5 32.8 %all-to-all-start = ((bf16[16,128,256]{2,1,0:T(8,128)(2,1)}), bf16[16,128,256]{2,1,0:T(8,128)(2,1)}, u32[]{:S(2)}, u32[]{:S(2)}) async-start(bf16[16,128,256]{2,1,0:T(8,128)(2,1)} %gather_fusion), calls=%async_computation | async-start | bytes 2097152 | tf_op jit(solution)/shard_map/all_to_all | solution.py:16
  27.7 0.7 copy-start.6
  37.4 5.9 %copy-start.2 = (f32[20,128,256]{2,1,0:T(8,128)}, f32[20,128,256]{2,1,0:T(8,128)S(1)}, u32[]{:S(2)}) copy-start(f32[20,128,256]{2,1,0:T(8,128)S(1)} %scatter_fusion.1) | copy-start | bytes 7864324
  39.2 10.2 %copy-start.3 = (bf16[512,256]{1,0:T(8,128)(2,1)S(1)}, bf16[512,256]{1,0:T(8,128)(2,1)}, u32[]{:S(2)}) copy-start(bf16[512,256]{1,0:T(8,128)(2,1)} %param.8) | copy-start | bytes 786436
  43.3 47.9 %all-to-all-start.1 = ((f32[16,128,256]{2,1,0:T(8,128)}), f32[16,128,256]{2,1,0:T(8,128)}, u32[]{:S(2)}, u32[]{:S(2)}) async-start(f32[16,128,256]{2,1,0:T(8,128)} %slice.15), calls=%async_computation.2 | async-start | bytes 4194304 | tf_op jit(solution)/shard_map/all_to_all | solution.py:37
  49.3 28.8 %reduce-scatter.3.cloned.1.call-start = ((), (), s32[]{:S(2)}) async-start(), calls=%async_computation.4 | async-start | bytes 1572864 | tf_op jit(solution)/shard_map/reduce_scatter | solution.py:24
  50.7 2.4 %copy-start.4 = (bf16[40,128,128]{2,1,0:T(8,128)(2,1)S(1)}, bf16[40,128,128]{2,1,0:T(8,128)(2,1)}, u32[]{:S(2)}) copy-start(bf16[40,128,128]{2,1,0:T(8,128)(2,1)} %param.11) | copy-start | bytes 3932164
  67.2 1.1 copy-start.1
  67.2 24.0 %copy-start.8 = (s32[1,16]{1,0:T(1,128)S(1)}, s32[1,16]{1,0:T(1,128)}, u32[]{:S(2)}) copy-start(s32[1,16]{1,0:T(1,128)} %param.15) | copy-start | bytes 196
  68.3 27.1 %reduce-scatter.5.cloned.1.call-start = ((), (), s32[]{:S(2)}) async-start(), calls=%async_computation.5 | async-start | bytes 393216 | tf_op jit(solution)/shard_map/reduce_scatter | solution.py:46
  80.1 125.0 %all-reduce.2.cloned.1.call-start = ((), (), s32[]{:S(2)}) async-start(), calls=%async_computation.6 | async-start | bytes 262144 | tf_op jit(solution)/shard_map/psum | solution.py:47
Sparse Core Ops, SparseCore 0:
  68.4 9.5 reduce-scatter.2
  80.9 8.9 reduce-scatter.4
  95.6 109.4 all-reduce.1
where the time goes:
time: 215 us
  waiting for transfers between devices  133 us (62%)
  other arithmetic  25.5 us (12%)
  between operations  14.6 us (7%)
  starting transfers between devices  14.4 us (7%)
  matrix products  12 us (6%)
  local copies, waits for them, and re-layouts  11.1 us (5%)
  blocking collectives  4.37 us (2%)
    psum x1, waiting for transfers between devices, local(): dom_share = lax.psum(col_share, 'dom')  109 us
    all_to_all x1, waiting for transfers between devices, local(): lax.all_to_all(spread[half_blocks:], 'dom', split_axis=0, concat_axis=0,...  9.96 us
    reduce_scatter x1, waiting for transfers between devices, local(): lax.psum_scatter(partial_value, 'col', scatter_dimension=0, tiled=True)  9.7 us
    scatter-add x1, other arithmetic, local(): jax.ops.segment_sum(back_terms, tile_cols, num_segments=half_blocks + pee...  9.07 us
    scatter-add x1, other arithmetic, local(): jax.ops.segment_sum(products, tile_rows, num_segments=all_blocks)  9.04 us
    all_to_all x1, starting transfers between devices, local(): lax.all_to_all(outgoing, 'dom', split_axis=0, concat_axis=0, tiled=True)  8.39 us
    all_to_all x1, starting transfers between devices, local(): lax.all_to_all(spread[half_blocks:], 'dom', split_axis=0, concat_axis=0,...  5.93 us
    dot_general x1, matrix products, local(): jnp.einsum('tij,tjf->tif', masked_tiles, picked, preferred_element_type=j...  4.93 us
  transfers between devices with their start and end apart: 5, of which 4 were waited for; matrix products, arithmetic and copies ran while one was open for 20% of the time, Pallas kernels for 0%

commit v1 on v0

v1 whole, which is shorter than its diff:
```python
import functools

import jax
import jax.numpy as jnp
from jax import lax
from jax.experimental import pallas as pl
from jax.experimental.pallas import tpu as pltpu
from jax.sharding import PartitionSpec as P

MESH = pl.DeviceIdType.MESH
F32 = jnp.float32


def kernel(scale, rows_s, cols_s, count_s, send_s, feat, weight, cot, tiles_hbm,
           out, fgrad, wgrad,
           tiles, sendf, recvf, sendb, recvb, buf, base, gh, psend, precv, hid,
           wsend, wrecv, wchunk, wpart, wall, wpeer, tos,
           f_send, f_recv, b_send, b_recv, r_send, r_recv, g_send, g_recv, misc):
    slots = tiles.shape[0]
    half, blk, width = feat.shape
    n = recvf.shape[0]
    blocks = 2 * half
    me = lax.axis_index("dom")
    col = lax.axis_index("col")
    other = 1 - col
    count = count_s[0]

    def to_peer(k):
        return lax.rem(me + k, n)

    def from_peer(k):
        return lax.rem(me + n - k, n)

    def remote(src, dst, s_sem, r_sem, dom, core):
        return pltpu.make_async_remote_copy(
            src_ref=src, dst_ref=dst, send_sem=s_sem, recv_sem=r_sem,
            device_id=(dom, core), device_id_type=MESH)

    tile_copy = pltpu.make_async_copy(tiles_hbm, tiles, misc.at[0])
    tile_copy.start()

    barrier = pltpu.get_barrier_semaphore()

    def greet(k, carry):
        pl.semaphore_signal(barrier, inc=1, device_id=(to_peer(k), col), device_id_type=MESH)
        return carry

    lax.fori_loop(1, n, greet, 0)
    pl.semaphore_signal(barrier, inc=1, device_id=(me, other), device_id_type=MESH)

    def gather(k, carry):
        sendf[k] = feat[send_s[to_peer(k)]]
        return carry

    lax.fori_loop(1, n, gather, 0)
    recvf[me] = feat[send_s[me]]

    own = lax.dot_general(cot[...], weight[...], (((1,), (1,)), ((), ())),
                          preferred_element_type=F32).astype(jnp.bfloat16)
    gh[pl.ds(col * half, half)] = own.reshape(half, blk, width)

    def find(s, carry):
        found = jnp.int32(0)
        for t in range(slots):
            found = jnp.where((cols_s[t] == s + half) & (t < count), t + 1, found)
        tos[s] = found
        return carry

    lax.fori_loop(0, n, find, 0)

    pl.semaphore_wait(barrier, n)

    def f_copy(k, peer, slot):
        return remote(sendf.at[k], recvf.at[slot], f_send.at[k], f_recv.at[slot], peer, col)

    def b_copy(k, peer, slot):
        return remote(sendb.at[k], recvb.at[slot], b_send.at[k], b_recv.at[slot], peer, col)

    gh_half = gh.at[pl.ds(col * half, half)]
    gh_copy = remote(gh_half, gh_half, misc.at[1], misc.at[2], me, other)
    gh_copy.start()

    def f_start(k, carry):
        f_copy(k, to_peer(k), me).start()
        return carry

    lax.fori_loop(1, n, f_start, 0)

    buf[0] = jnp.zeros((blk, width), F32)
    tile_copy.wait()
    gh_copy.wait_send()
    gh_other = gh.at[pl.ds(other * half, half)]
    remote(gh_other, gh_other, misc.at[1], misc.at[2], me, other).wait_recv()

    def back_term(slot):
        found = tos[slot]
        at = jnp.maximum(found - 1, 0)
        term = lax.dot_general(tiles[at], gh[rows_s[at]], (((0,), (0,)), ((), ())),
                               preferred_element_type=F32)
        return jnp.where(found > 0, term, 0.0).astype(jnp.bfloat16)

    def b_start(k, carry):
        sendb[k] = back_term(to_peer(k))
        b_copy(k, to_peer(k), me).start()
        return carry

    lax.fori_loop(1, n, b_start, 0)
    recvb[me] = back_term(me)

    def link(lasts, key, index):
        prev = jnp.int32(0)
        for r, last in enumerate(lasts):
            prev = jnp.where(key == r, last, prev)
        return prev, tuple(jnp.where(key == r, index, last) for r, last in enumerate(lasts))

    def own_back(t, lasts):
        key = jnp.where(t < count, cols_s[t], -1)
        prev, lasts = link(lasts, key, t + 1)
        term = lax.dot_general(tiles[t], gh[rows_s[t]], (((0,), (0,)), ((), ())),
                               preferred_element_type=F32)
        buf[t + 1] = buf[prev] + term
        return lasts

    lasts = lax.fori_loop(0, slots, own_back, (jnp.int32(0),) * half)
    for j in range(half):
        base[j] = buf[lasts[j]]

    def own_fwd(t, lasts):
        source = cols_s[t]
        key = jnp.where((t < count) & (source < half), rows_s[t], -1)
        prev, lasts = link(lasts, key, t + 1)
        term = jnp.dot(tiles[t], feat[jnp.minimum(source, half - 1)], preferred_element_type=F32)
        buf[t + 1] = buf[prev] + term
        return lasts

    lasts = lax.fori_loop(0, slots, own_fwd, (jnp.int32(0),) * blocks)

    def slot_fwd(k, slot, lasts):
        found = tos[slot]
        at = jnp.maximum(found - 1, 0)
        key = jnp.where(found > 0, rows_s[at], -1)
        prev, lasts = link(lasts, key, slots + 1 + k)
        term = jnp.dot(tiles[at], recvf[slot], preferred_element_type=F32)
        buf[slots + 1 + k] = buf[prev] + term
        return lasts

    lasts = slot_fwd(0, me, lasts)

    def arrived(k, lasts):
        f_copy(k, from_peer(k), from_peer(k)).wait_recv()
        return slot_fwd(k, from_peer(k), lasts)

    lasts = lax.fori_loop(1, n, arrived, lasts)

    for j in range(half):
        psend[j] = buf[jnp.where(col == 0, lasts[half + j], lasts[j])]
    p_copy = remote(psend, precv, misc.at[3], misc.at[4], me, other)
    p_copy.start()
    p_copy.wait()
    for j in range(half):
        mine = buf[jnp.where(col == 0, lasts[j], lasts[half + j])]
        hid[pl.ds(j * blk, blk), :] = (mine + precv[j]).astype(jnp.bfloat16)

    local = lax.dot_general(hid[...], cot[...], (((0,), (0,)), ((), ())),
                            preferred_element_type=F32) * jnp.float32(scale)
    wh = width // 2
    low, high = local[:wh], local[wh:]
    wsend[...] = jnp.where(col == 0, high, low)
    w_copy = remote(wsend, wrecv, misc.at[5], misc.at[6], me, other)
    w_copy.start()
    out[...] = jnp.dot(hid[...], weight[...], preferred_element_type=F32).astype(jnp.bfloat16)
    w_copy.wait()
    share = jnp.where(col == 0, low, high) + wrecv[...]
    wchunk[...] = share.reshape(wchunk.shape)

    def r_copy(peer, chunk, slot):
        return remote(wchunk.at[chunk], wpart.at[slot], r_send.at[chunk], r_recv.at[slot], peer, col)

    def r_start(k, carry):
        r_copy(to_peer(k), to_peer(k), me).start()
        return carry

    lax.fori_loop(1, n, r_start, 0)
    wpart[me] = wchunk[me]

    def r_wait(k, carry):
        r_copy(from_peer(k), from_peer(k), from_peer(k)).wait_recv()
        return carry

    lax.fori_loop(1, n, r_wait, 0)
    wall[me] = jnp.sum(wpart[...], axis=0)

    def g_copy(k, peer, slot):
        return remote(wall.at[slot], wall.at[slot], g_send.at[k], g_recv.at[slot], peer, col)

    def g_start(k, carry):
        g_copy(k, to_peer(k), me).start()
        return carry

    lax.fori_loop(1, n, g_start, 0)

    def b_wait(k, carry):
        b_copy(k, from_peer(k), from_peer(k)).wait_recv()
        return carry

    lax.fori_loop(1, n, b_wait, 0)
    step = 16

    def total(i, carry):
        at = pl.ds(pl.multiple_of(i * step, step), step)

        def add(s, sums):
            value = recvb[s, at, :].astype(F32)
            home = send_s[s]
            return tuple(acc + jnp.where(home == j, value, 0.0) for j, acc in enumerate(sums))

        sums = lax.fori_loop(0, n, add, tuple(base[j, at, :] for j in range(half)), unroll=4)
        for j in range(half):
            fgrad[j, at, :] = sums[j].astype(jnp.bfloat16)
        return carry

    lax.fori_loop(0, blk // step, total, 0)

    def g_wait(k, carry):
        g_copy(k, from_peer(k), from_peer(k)).wait_recv()
        return carry

    lax.fori_loop(1, n, g_wait, 0)
    x_copy = remote(wall, wpeer, misc.at[7], misc.at[8], me, other)
    x_copy.start()

    def drain(k, carry):
        f_copy(k, to_peer(k), me).wait_send()
        b_copy(k, to_peer(k), me).wait_send()
        r_copy(to_peer(k), to_peer(k), me).wait_send()
        g_copy(k, to_peer(k), me).wait_send()
        return carry

    lax.fori_loop(1, n, drain, 0)
    wgrad[pl.ds(pl.multiple_of(col * wh, wh), wh), :] = wall[...].reshape(wh, wgrad.shape[1])
    x_copy.wait()
    wgrad[pl.ds(pl.multiple_of(other * wh, wh), wh), :] = wpeer[...].reshape(wh, wgrad.shape[1])


def local(features, weight, cotangent, tile_values, tile_rows, tile_cols, tile_count, send_blocks):
    slots, blk, _ = tile_values.shape
    rows, width = features.shape
    width_out = cotangent.shape[1]
    half = rows // blk
    n = send_blocks.shape[1]
    nodes = rows * lax.axis_size("col") * lax.axis_size("dom")
    scale = 1.0 / nodes**0.5
    bf = jnp.bfloat16
    chunk = width // 2 // n
    vmem = pl.BlockSpec(memory_space=pltpu.VMEM)
    smem = pl.BlockSpec(memory_space=pltpu.SMEM)
    sems = pltpu.SemaphoreType.DMA
    out, fgrad, wgrad = pl.pallas_call(
        functools.partial(kernel, scale),
        out_shape=(
            jax.ShapeDtypeStruct((rows, width_out), bf),
            jax.ShapeDtypeStruct((half, blk, width), bf),
            jax.ShapeDtypeStruct((width, width_out), F32),
        ),
        in_specs=[smem] * 4 + [vmem] * 3 + [pl.BlockSpec(memory_space=pl.ANY)],
        out_specs=(vmem, vmem, vmem),
        scratch_shapes=[
            pltpu.VMEM((slots, blk, blk), bf),
            pltpu.VMEM((n, blk, width), bf),
            pltpu.VMEM((n, blk, width), bf),
            pltpu.VMEM((n, blk, width), bf),
            pltpu.VMEM((n, blk, width), bf),
            pltpu.VMEM((slots + 1 + n, blk, width), F32),
            pltpu.VMEM((half, blk, width), F32),
            pltpu.VMEM((2 * half, blk, width), bf),
            pltpu.VMEM((half, blk, width), F32),
            pltpu.VMEM((half, blk, width), F32),
            pltpu.VMEM((rows, width), bf),
            pltpu.VMEM((width // 2, width_out), F32),
            pltpu.VMEM((width // 2, width_out), F32),
            pltpu.VMEM((n, chunk, width_out), F32),
            pltpu.VMEM((n, chunk, width_out), F32),
            pltpu.VMEM((n, chunk, width_out), F32),
            pltpu.VMEM((n, chunk, width_out), F32),
            pltpu.SMEM((n,), jnp.int32),
        ] + [sems((n,))] * 8 + [sems((9,))],
        compiler_params=pltpu.CompilerParams(
            collective_id=0, has_side_effects=True, vmem_limit_bytes=67000000),
    )(tile_rows, tile_cols, tile_count, send_blocks.reshape(n),
      features.reshape(half, blk, width), weight, cotangent, tile_values)
    return out, fgrad.reshape(rows, width), wgrad


def solution(mesh):
    return jax.shard_map(
        local,
        mesh=mesh,
        in_specs=(
            P(("dom", "col"), None),
            P(),
            P(("dom", "col"), None),
            P(("dom", "col"), None, None),
            P(("dom", "col")),
            P(("dom", "col")),
            P(("dom", "col")),
            P(("dom", "col"), None),
        ),
        out_specs=(P(("dom", "col"), None), P(("dom", "col"), None), P()),
        check_vma=False,
    )
```

time: 215 us -> 72.4 us (0.34)
  waiting for transfers between devices: 133 us -> 0 us
  Pallas kernels: 0 us -> 65.8 us
  other arithmetic: 25.5 us -> 0 us
  starting transfers between devices: 14.4 us -> 0 us
  between operations: 14.6 us -> 1.29 us
  matrix products: 12 us -> 0 us
  local copies, waits for them, and re-layouts: 11.1 us -> 5.01 us
  blocking collectives: 4.37 us -> 0 us
    psum x1 -> x0, waiting for transfers between devices: 109 us -> none  [local(): dom_share = lax.psum(col_share, 'dom')]
    pallas_call x0 -> x1, Pallas kernels: none -> 65.8 us  [local(): pl.pallas_call(functools.partial(kernel, scale), out_shape=(jax.ShapeDtyp...]
    scatter-add x3 -> x0, other arithmetic: 21.6 us -> none  [the longest x1 9.07 us: local(): jax.ops.segment_sum(back_terms, tile_cols, num_segments=half_blocks + pee...]
    all_to_all x2 -> x0, starting transfers between devices: 14.3 us -> none  [the longest x1 8.39 us: local(): lax.all_to_all(outgoing, 'dom', split_axis=0, concat_axis=0, tiled=True)]
    all_to_all x2 -> x0, waiting for transfers between devices: 14.1 us -> none  [the longest x1 9.96 us: local(): lax.all_to_all(spread[half_blocks:], 'dom', split_axis=0, concat_axis=0,...]
    dot_general x5 -> x0, matrix products: 12 us -> none  [the longest x1 4.93 us: local(): jnp.einsum('tij,tjf->tif', masked_tiles, picked, preferred_element_type=j...]
    reduce_scatter x2 -> x0, waiting for transfers between devices: 9.71 us -> none  [the longest x1 9.7 us: local(): lax.psum_scatter(partial_value, 'col', scatter_dimension=0, tiled=True)]
    gather x3 -> x0, local copies, waits for them, and re-layouts: 5.7 us -> none  [the longest x1 2.58 us: local(): outgoing = own_blocks[send_blocks[0]]]
  transfers between devices with their start and end apart: 5 -> 0, of which waited for: 4 -> 0; matrix products, arithmetic and copies ran while one was open for 20% -> 0% of each run, Pallas kernels for 0% -> 0%
where the time goes in v1:
time: 72.4 us; the launch traced here: 72.1 us
  Pallas kernels  65.8 us (91%)
  local copies, waits for them, and re-layouts  5.01 us (7%)
  between operations  1.29 us (2%)
    pallas_call x1, Pallas kernels, local(): pl.pallas_call(functools.partial(kernel, scale), out_shape=(jax.ShapeDtyp...  65.8 us
    unnamed x3, local copies, waits for them, and re-layouts  5.01 us

profile of v1, /device:TPU:0, one launch (start us, length us, event | category | flops | bytes accessed | tf_op | source)
XLA Modules:
  0.0 72.1 jit_solution(13775723152598653179)
XLA Ops:
  1.3 65.8 %shard_map.103 = (bf16[512,256]{1,0:T(8,128)(2,1)}, bf16[4,128,256]{2,1,0:T(8,128)(2,1)}, f32[256,256]{1,0:T(8,128)}) custom-call(s32[40]{0:T(128)} %rows_s.1, s32[40]{0:T(128)} %cols_s.1, s32[1]{0:T(128)S(6)} %copy.14.count_s, s32[16]{0:T(128)} %bitcast.5, bf16[4,128,256]{2,1,0:T(8,128)(2,1)} %bitcast.3, bf16[256,256]{1,0:T(8,128)(2,1)} %weight.1, ...), custom_call_target="tpu_custom_call" | custom-call | tf_op jit(solution)/shard_map/pallas_call | solution.py:258
  67.1 1.7 %copy.15 = bf16[512,256]{1,0:T(8,128)(2,1)} copy(bf16[512,256]{1,0:T(8,128)(2,1)} %get-tuple-element.12) | data formatting | bytes 524288
  68.8 1.7 %copy.16 = bf16[512,256]{1,0:T(8,128)(2,1)} copy(bf16[512,256]{1,0:T(8,128)(2,1)} %bitcast.4) | data formatting | bytes 524288
  70.5 1.7 %copy.17 = f32[256,256]{1,0:T(8,128)} copy(f32[256,256]{1,0:T(8,128)} %get-tuple-element.14) | data formatting | bytes 524288

commit v2 on v1

--- a/solution.py
+++ b/solution.py
@@ -11,9 +11,9 @@
 F32 = jnp.float32
 
 
-def kernel(scale, rows_s, cols_s, count_s, send_s, feat, weight, cot, tiles_hbm,
+def kernel(scale, rows_s, cols_s, count_s, send_s, feat_hbm, weight_hbm, cot_hbm, tiles_hbm,
            out, fgrad, wgrad,
-           tiles, sendf, recvf, sendb, recvb, buf, base, gh, psend, precv, hid,
+           feat, weight, cot, tiles, sendf, recvf, sendb, recvb, buf, base, gh, psend, precv, hid,
            wsend, wrecv, wchunk, wpart, wall, wpeer, tos,
            f_send, f_recv, b_send, b_recv, r_send, r_recv, g_send, g_recv, misc):
     slots = tiles.shape[0]
@@ -25,17 +25,29 @@
     other = 1 - col
     count = count_s[0]
 
+    side = n // 2
+    mine_side, spot = lax.div(me, side), lax.rem(me, side)
+
+    def peer_side(k):
+        return lax.rem(mine_side + 1 + lax.div(k - 1, side), 2) * side
+
     def to_peer(k):
-        return lax.rem(me + k, n)
+        return peer_side(k) + lax.rem(spot + k, side)
 
     def from_peer(k):
-        return lax.rem(me + n - k, n)
+        return peer_side(k) + lax.rem(spot + 2 * side - k, side)
 
     def remote(src, dst, s_sem, r_sem, dom, core):
         return pltpu.make_async_remote_copy(
             src_ref=src, dst_ref=dst, send_sem=s_sem, recv_sem=r_sem,
             device_id=(dom, core), device_id_type=MESH)
 
+    feat_copy = pltpu.make_async_copy(feat_hbm, feat, misc.at[9])
+    feat_copy.start()
+    cot_copy = pltpu.make_async_copy(cot_hbm, cot, misc.at[10])
+    cot_copy.start()
+    weight_copy = pltpu.make_async_copy(weight_hbm, weight, misc.at[11])
+    weight_copy.start()
     tile_copy = pltpu.make_async_copy(tiles_hbm, tiles, misc.at[0])
     tile_copy.start()
 
@@ -48,6 +60,8 @@
     lax.fori_loop(1, n, greet, 0)
     pl.semaphore_signal(barrier, inc=1, device_id=(me, other), device_id_type=MESH)
 
+    feat_copy.wait()
+
     def gather(k, carry):
         sendf[k] = feat[send_s[to_peer(k)]]
         return carry
@@ -55,6 +69,8 @@
     lax.fori_loop(1, n, gather, 0)
     recvf[me] = feat[send_s[me]]
 
+    cot_copy.wait()
+    weight_copy.wait()
     own = lax.dot_general(cot[...], weight[...], (((1,), (1,)), ((), ())),
                           preferred_element_type=F32).astype(jnp.bfloat16)
     gh[pl.ds(col * half, half)] = own.reshape(half, blk, width)
@@ -99,12 +115,24 @@
                                preferred_element_type=F32)
         return jnp.where(found > 0, term, 0.0).astype(jnp.bfloat16)
 
+    def b_fill(k, carry):
+        sendb[k] = back_term(to_peer(k))
+        return carry
+
+    lax.fori_loop(1, n, b_fill, 0)
+
     def b_start(k, carry):
-        sendb[k] = back_term(to_peer(k))
         b_copy(k, to_peer(k), me).start()
         return carry
 
-    lax.fori_loop(1, n, b_start, 0)
+    cut1, cut2 = 1 + side // 2, 1 + 3 * side // 4
+    ends = (1, cut1, cut2, side + 1)
+    side_ends = (side + 1, side + side // 2, side + 3 * side // 4, n)
+
+    def b_part(i):
+        lax.fori_loop(ends[i], ends[i + 1], b_start, 0)
+        lax.fori_loop(side_ends[i], side_ends[i + 1], b_start, 0)
+
     recvb[me] = back_term(me)
 
     def link(lasts, key, index):
@@ -134,6 +162,8 @@
         return lasts
 
     lasts = lax.fori_loop(0, slots, own_fwd, (jnp.int32(0),) * blocks)
+
+    b_part(0)
 
     def slot_fwd(k, slot, lasts):
         found = tos[slot]
@@ -146,7 +176,8 @@
 
     lasts = slot_fwd(0, me, lasts)
 
-    def arrived(k, lasts):
+    def arrived(i, lasts):
+        k = n - i
         f_copy(k, from_peer(k), from_peer(k)).wait_recv()
         return slot_fwd(k, from_peer(k), lasts)
 
@@ -181,6 +212,7 @@
         return carry
 
     lax.fori_loop(1, n, r_start, 0)
+    b_part(1)
     wpart[me] = wchunk[me]
 
     def r_wait(k, carry):
@@ -198,6 +230,16 @@
         return carry
 
     lax.fori_loop(1, n, g_start, 0)
+    b_part(2)
+
+    def g_wait(k, carry):
+        g_copy(k, from_peer(k), from_peer(k)).wait_recv()
+        return carry
+
+    lax.fori_loop(1, n, g_wait, 0)
+    x_copy = remote(wall, wpeer, misc.at[7], misc.at[8], me, other)
+    x_copy.start()
+    wgrad[pl.ds(pl.multiple_of(col * wh, wh), wh), :] = wall[...].reshape(wh, wgrad.shape[1])
 
     def b_wait(k, carry):
         b_copy(k, from_peer(k), from_peer(k)).wait_recv()
@@ -220,14 +262,6 @@
         return carry
 
     lax.fori_loop(0, blk // step, total, 0)
-
-    def g_wait(k, carry):
-        g_copy(k, from_peer(k), from_peer(k)).wait_recv()
-        return carry
-
-    lax.fori_loop(1, n, g_wait, 0)
-    x_copy = remote(wall, wpeer, misc.at[7], misc.at[8], me, other)
-    x_copy.start()
 
     def drain(k, carry):
         f_copy(k, to_peer(k), me).wait_send()
@@ -237,9 +271,34 @@
         return carry
 
     lax.fori_loop(1, n, drain, 0)
-    wgrad[pl.ds(pl.multiple_of(col * wh, wh), wh), :] = wall[...].reshape(wh, wgrad.shape[1])
     x_copy.wait()
     wgrad[pl.ds(pl.multiple_of(other * wh, wh), wh), :] = wpeer[...].reshape(wh, wgrad.shape[1])
+
+
+def place(*refs):
+    count = (len(refs) - 1) // 3
+    sources, targets, held, sem = refs[:count], refs[count:2 * count], refs[2 * count:-1], refs[-1]
+    reads = [pltpu.make_async_copy(a, h, sem.at[i]) for i, (a, h) in enumerate(zip(sources, held))]
+    writes = [pltpu.make_async_copy(h, b, sem.at[count + i]) for i, (h, b) in enumerate(zip(held, targets))]
+    for read in reads:
+        read.start()
+    for read, write in zip(reads, writes):
+        read.wait()
+        write.start()
+    for write in writes:
+        write.wait()
+
+
+def finish(*arrays):
+    hbm = pl.BlockSpec(memory_space=pl.ANY)
+    return pl.pallas_call(
+        place,
+        out_shape=tuple(jax.ShapeDtypeStruct(a.shape, a.dtype) for a in arrays),
+        in_specs=[hbm] * len(arrays),
+        out_specs=(hbm,) * len(arrays),
+        scratch_shapes=[pltpu.VMEM(a.shape, a.dtype) for a in arrays]
+        + [pltpu.SemaphoreType.DMA((2 * len(arrays),))],
+    )(*arrays)
 
 
 def local(features, weight, cotangent, tile_values, tile_rows, tile_cols, tile_count, send_blocks):
@@ -253,6 +312,7 @@
     bf = jnp.bfloat16
     chunk = width // 2 // n
     vmem = pl.BlockSpec(memory_space=pltpu.VMEM)
+    hbm = pl.BlockSpec(memory_space=pl.ANY)
     smem = pl.BlockSpec(memory_space=pltpu.SMEM)
     sems = pltpu.SemaphoreType.DMA
     out, fgrad, wgrad = pl.pallas_call(
@@ -262,9 +322,12 @@
             jax.ShapeDtypeStruct((half, blk, width), bf),
             jax.ShapeDtypeStruct((width, width_out), F32),
         ),
-        in_specs=[smem] * 4 + [vmem] * 3 + [pl.BlockSpec(memory_space=pl.ANY)],
+        in_specs=[smem] * 4 + [hbm] * 4,
         out_specs=(vmem, vmem, vmem),
         scratch_shapes=[
+            pltpu.VMEM((half, blk, width), bf),
+            pltpu.VMEM((width, width_out), bf),
+            pltpu.VMEM((rows, width_out), bf),
             pltpu.VMEM((slots, blk, blk), bf),
             pltpu.VMEM((n, blk, width), bf),
             pltpu.VMEM((n, blk, width), bf),
@@ -283,12 +346,12 @@
             pltpu.VMEM((n, chunk, width_out), F32),
             pltpu.VMEM((n, chunk, width_out), F32),
             pltpu.SMEM((n,), jnp.int32),
-        ] + [sems((n,))] * 8 + [sems((9,))],
+        ] + [sems((n,))] * 8 + [sems((12,))],
         compiler_params=pltpu.CompilerParams(
             collective_id=0, has_side_effects=True, vmem_limit_bytes=67000000),
     )(tile_rows, tile_cols, tile_count, send_blocks.reshape(n),
       features.reshape(half, blk, width), weight, cotangent, tile_values)
-    return out, fgrad.reshape(rows, width), wgrad
+    return finish(out, fgrad.reshape(rows, width), wgrad)
 
 
 def solution(mesh):

time: 72.4 us -> 66.8 us (0.923)
  local copies, waits for them, and re-layouts: 5.01 us -> 0 us
    unnamed x3 -> x0, local copies, waits for them, and re-layouts: 5.01 us -> none
    pallas_call x1, Pallas kernels: 65.8 us -> 63.5 us  [local(): pl.pallas_call(functools.partial(kernel, scale), out_shape=(jax.ShapeDtyp...]
    pallas_call x0 -> x1, Pallas kernels: none -> 1.88 us  [finish(): pl.pallas_call(place, out_shape=tuple((jax.ShapeDtypeStruct(a.shape, a.dt...]
where the time goes in v2:
time: 66.8 us; the launch traced here: 66.7 us
  Pallas kernels  65.4 us (98%)
  between operations  1.29 us (2%)
    pallas_call x1, Pallas kernels, local(): pl.pallas_call(functools.partial(kernel, scale), out_shape=(jax.ShapeDtyp...  63.5 us
    pallas_call x1, Pallas kernels, finish(): pl.pallas_call(place, out_shape=tuple((jax.ShapeDtypeStruct(a.shape, a.dt...  1.88 us

profile of v2, /device:TPU:0, one launch (start us, length us, event | category | flops | bytes accessed | tf_op | source)
XLA Modules:
  0.0 66.7 jit_solution(18354941132757374611)
XLA Ops:
  1.3 63.5 %shard_map.103 = (bf16[512,256]{1,0:T(8,128)(2,1)}, bf16[4,128,256]{2,1,0:T(8,128)(2,1)}, f32[256,256]{1,0:T(8,128)}) custom-call(s32[40]{0:T(128)} %rows_s.1, s32[40]{0:T(128)} %cols_s.1, s32[1]{0:T(128)S(6)} %copy.11.count_s, s32[16]{0:T(128)} %bitcast.5, bf16[4,128,256]{2,1,0:T(8,128)(2,1)} %bitcast.3, bf16[256,256]{1,0:T(8,128)(2,1)} %weight_hbm.1, ...), custom_call_target="tpu_custom_call" | custom-call | tf_op jit(solution)/shard_map/pallas_call | solution.py:318
  64.8 1.9 %shard_map.104 = (bf16[512,256]{1,0:T(8,128)(2,1)}, bf16[512,256]{1,0:T(8,128)(2,1)}, f32[256,256]{1,0:T(8,128)}) custom-call(bf16[512,256]{1,0:T(8,128)(2,1)} %get-tuple-element.6.refs_0_, bf16[512,256]{1,0:T(8,128)(2,1)} %bitcast.4, f32[256,256]{1,0:T(8,128)} %get-tuple-element.8.refs_2_), custom_call_target="tpu_custom_call" | custom-call | tf_op jit(solution)/shard_map/pallas_call | solution.py:294
